TPU v7x, 32 devices: a whole 2x2x4 slice. The times are simulated.
32 devices in a mesh: gy: 8 (over z, x), gx: 4 (over y, core).
Axes of the slice: x: 2, y: 2, z: 4, core: 2. Of those that a mesh axis runs over, the one named last changes fastest.
Arguments:
- fields: float32 [8, 64, 256, 128], P(None, 'gx', 'gy'), may hold values from -6 to 6
- shifts: int32 [64], P('gx'), may hold values from 0 to 255
- fraction: float32 [64], P('gx'), may hold values from 0.4 to 0.6
Outputs:
- remapped: float32 [8, 64, 256, 128], P(None, 'gx', 'gy')
- stress: float32 [2, 128], replicated
All inputs are finite; a program needn't handle non-finite values.
Results may differ from a plain program's by a relative error of at most 0.0003.
Values sent between devices are 32-bit elements; how exact they have to be, the bound alone decides.
A program may use at most 64 MiB of HBM per device.

v0:
```python
from functools import partial
import math

import jax
import jax.numpy as jnp
from jax import lax
from jax.sharding import PartitionSpec as P


def remap_cells(extended, fraction, length, stride):

    def cells(first, number):
        return extended[..., first * stride : (first + number) * stride]

    interface = (
        7.0 * (cells(1, length + 2) + cells(2, length + 2))
        - (cells(0, length + 2) + cells(3, length + 2))
    ) / 12.0
    left_edge = interface[..., : (length + 1) * stride]
    right_edge = interface[..., stride:]
    centre = cells(2, length + 1)
    slope = right_edge - left_edge
    curve = 6.0 * centre - 3.0 * (left_edge + right_edge)
    outflow = fraction * (
        right_edge - 0.5 * fraction * (slope - (1.0 - 2.0 * fraction / 3.0) * curve)
    )
    return cells(3, length) - outflow[..., stride:] + outflow[..., : length * stride]


def cut_flat(column, offset, length):
    return lax.dynamic_slice_in_dim(column, offset, length, 0)


def on_device(fields, shifts, fraction):
    components = fields.shape[0]
    columns = fields.shape[1]
    slab_cells = fields.shape[2]
    vertical = fields.shape[3]
    loop_size = lax.axis_size("gy")
    pair_count = components * columns
    stacked = fields.reshape(pair_count, slab_cells, vertical)
    gathered = lax.all_to_all(stacked, "gy", split_axis=0, concat_axis=1, tiled=True)
    held = gathered.shape[0]
    azimuth = gathered.shape[1]
    pair_ids = lax.axis_index("gy") * held + jnp.arange(held, dtype=jnp.int32)
    column_ids = jnp.mod(pair_ids, columns)
    picker = column_ids[:, None] == jnp.arange(columns, dtype=jnp.int32)[None, :]
    pair_shift = jnp.sum(jnp.where(picker, shifts[None, :], 0), axis=1)
    pair_share = jnp.sum(jnp.where(picker, fraction[None, :], 0.0), axis=1)
    flat = gathered.reshape(held, azimuth * vertical)
    doubled = jnp.concatenate([flat, flat, flat[:, : 4 * vertical]], axis=1)
    starts = jnp.mod(-3 - pair_shift, azimuth) * vertical
    cutter = partial(cut_flat, length=(azimuth + 5) * vertical)
    extended = jax.vmap(cutter, in_axes=(0, 0), out_axes=0)(doubled, starts)
    moved = remap_cells(extended, pair_share[:, None], azimuth, vertical).reshape(
        held, azimuth, vertical
    )
    returned = lax.all_to_all(moved, "gy", split_axis=1, concat_axis=0, tiled=True)
    remapped = returned.reshape(fields.shape)
    reynolds = jnp.sum(remapped[1] * remapped[2], axis=(0, 1))
    maxwell = -jnp.sum(remapped[5] * remapped[6], axis=(0, 1))
    partial_sums = jnp.stack([reynolds, maxwell])
    summed = lax.psum(partial_sums, ("gy", "gx"))
    total_cells = columns * lax.axis_size("gx") * slab_cells * loop_size
    stress = summed / math.sqrt(total_cells)
    return (remapped, stress)


def solution(mesh):
    in_specs = (P(None, "gx", "gy", None), P("gx"), P("gx"))
    out_specs = (P(None, "gx", "gy", None), P())
    return jax.shard_map(
        on_device, mesh=mesh, in_specs=in_specs, out_specs=out_specs, check_vma=False
    )
```

profile of v0, /device:TPU:0, one launch (start us, length us, event | category | flops | bytes accessed | tf_op | source)
XLA Modules:
  0.0 238.1 jit_solution(6908853262675557215)
XLA Ops:
  0.6 7.4 %all-to-all-start = ((f32[128,32,128]{2,1,0:T(8,128)}), f32[128,32,128]{2,1,0:T(8,128)}, u32[]{:S(2)}, u32[]{:S(2)}) async-start(f32[128,32,128]{2,1,0:T(8,128)} %bitcast.34), calls=%async_computation | async-start | bytes 4194304 | tf_op jit(solution)/shard_map/all_to_all | solution.py:42
  8.5 47.9 %all-to-all-done = f32[128,32,128]{2,1,0:T(8,128)} async-done(((f32[128,32,128]{2,1,0:T(8,128)}), f32[128,32,128]{2,1,0:T(8,128)}, u32[]{:S(2)}, u32[]{:S(2)}) %all-to-all-start) | async-done | bytes 2097184 | tf_op jit(solution)/shard_map/all_to_all | solution.py:42
  56.4 1.8 copy.15
  59.5 2.2 pad_maximum_fusion
  61.7 81.2 %while.1 = (s32[]{:T(128)}, f32[16,66048]{1,0:T(8,128)}, s32[16,2]{0,1:T(2,128)S(1)}, f32[16,33408]{1,0:T(8,128)S(1)}, s32[]{:T(128)}, /*index=5*/s32[]{:T(128)}) while((s32[]{:T(128)}, f32[16,66048]{1,0:T(8,128)}, s32[16,2]{0,1:T(2,128)S(1)}, f32[16,33408]{1,0:T(8,128)S(1)}, s32[]{:T(128)}, /*index=5*/s32[]{:T(128)}) %tuple.30), condition=%wide.while_cond, body=%wide.while_body.sunk | while | flops 2 | bytes 534641 | solution.py:31
  62.3 2.9 %dynamic-slice.7 = f32[1,33408]{1,0:T(1,128)S(1)} dynamic-slice(f32[16,66048]{1,0:T(8,128)} %get-tuple-element.76, s32[]{:T(128)} %bitcast.27, s32[]{:T(128)} %bitcast.28), dynamic_slice_sizes={1,33408} | dynamic-slice | bytes 267268 | tf_op jit(solution)/shard_map/vmap()/gather
  67.4 2.9 %dynamic-slice.7 = f32[1,33408]{1,0:T(1,128)S(1)} dynamic-slice(f32[16,66048]{1,0:T(8,128)} %get-tuple-element.76, s32[]{:T(128)} %bitcast.27, s32[]{:T(128)} %bitcast.28), dynamic_slice_sizes={1,33408} | dynamic-slice | bytes 267268 | tf_op jit(solution)/shard_map/vmap()/gather
  72.5 2.9 %dynamic-slice.7 = f32[1,33408]{1,0:T(1,128)S(1)} dynamic-slice(f32[16,66048]{1,0:T(8,128)} %get-tuple-element.76, s32[]{:T(128)} %bitcast.27, s32[]{:T(128)} %bitcast.28), dynamic_slice_sizes={1,33408} | dynamic-slice | bytes 267268 | tf_op jit(solution)/shard_map/vmap()/gather
  77.6 2.9 %dynamic-slice.7 = f32[1,33408]{1,0:T(1,128)S(1)} dynamic-slice(f32[16,66048]{1,0:T(8,128)} %get-tuple-element.76, s32[]{:T(128)} %bitcast.27, s32[]{:T(128)} %bitcast.28), dynamic_slice_sizes={1,33408} | dynamic-slice | bytes 267268 | tf_op jit(solution)/shard_map/vmap()/gather
  82.7 2.9 %dynamic-slice.7 = f32[1,33408]{1,0:T(1,128)S(1)} dynamic-slice(f32[16,66048]{1,0:T(8,128)} %get-tuple-element.76, s32[]{:T(128)} %bitcast.27, s32[]{:T(128)} %bitcast.28), dynamic_slice_sizes={1,33408} | dynamic-slice | bytes 267268 | tf_op jit(solution)/shard_map/vmap()/gather
  87.7 2.9 %dynamic-slice.7 = f32[1,33408]{1,0:T(1,128)S(1)} dynamic-slice(f32[16,66048]{1,0:T(8,128)} %get-tuple-element.76, s32[]{:T(128)} %bitcast.27, s32[]{:T(128)} %bitcast.28), dynamic_slice_sizes={1,33408} | dynamic-slice | bytes 267268 | tf_op jit(solution)/shard_map/vmap()/gather
  92.8 2.9 %dynamic-slice.7 = f32[1,33408]{1,0:T(1,128)S(1)} dynamic-slice(f32[16,66048]{1,0:T(8,128)} %get-tuple-element.76, s32[]{:T(128)} %bitcast.27, s32[]{:T(128)} %bitcast.28), dynamic_slice_sizes={1,33408} | dynamic-slice | bytes 267268 | tf_op jit(solution)/shard_map/vmap()/gather
  97.9 2.9 %dynamic-slice.7 = f32[1,33408]{1,0:T(1,128)S(1)} dynamic-slice(f32[16,66048]{1,0:T(8,128)} %get-tuple-element.76, s32[]{:T(128)} %bitcast.27, s32[]{:T(128)} %bitcast.28), dynamic_slice_sizes={1,33408} | dynamic-slice | bytes 267268 | tf_op jit(solution)/shard_map/vmap()/gather
  103.0 2.9 %dynamic-slice.7 = f32[1,33408]{1,0:T(1,128)S(1)} dynamic-slice(f32[16,66048]{1,0:T(8,128)} %get-tuple-element.76, s32[]{:T(128)} %bitcast.27, s32[]{:T(128)} %bitcast.28), dynamic_slice_sizes={1,33408} | dynamic-slice | bytes 267268 | tf_op jit(solution)/shard_map/vmap()/gather
  108.0 2.9 %dynamic-slice.7 = f32[1,33408]{1,0:T(1,128)S(1)} dynamic-slice(f32[16,66048]{1,0:T(8,128)} %get-tuple-element.76, s32[]{:T(128)} %bitcast.27, s32[]{:T(128)} %bitcast.28), dynamic_slice_sizes={1,33408} | dynamic-slice | bytes 267268 | tf_op jit(solution)/shard_map/vmap()/gather
  113.1 2.9 %dynamic-slice.7 = f32[1,33408]{1,0:T(1,128)S(1)} dynamic-slice(f32[16,66048]{1,0:T(8,128)} %get-tuple-element.76, s32[]{:T(128)} %bitcast.27, s32[]{:T(128)} %bitcast.28), dynamic_slice_sizes={1,33408} | dynamic-slice | bytes 267268 | tf_op jit(solution)/shard_map/vmap()/gather
  118.2 2.9 %dynamic-slice.7 = f32[1,33408]{1,0:T(1,128)S(1)} dynamic-slice(f32[16,66048]{1,0:T(8,128)} %get-tuple-element.76, s32[]{:T(128)} %bitcast.27, s32[]{:T(128)} %bitcast.28), dynamic_slice_sizes={1,33408} | dynamic-slice | bytes 267268 | tf_op jit(solution)/shard_map/vmap()/gather
  123.3 2.9 %dynamic-slice.7 = f32[1,33408]{1,0:T(1,128)S(1)} dynamic-slice(f32[16,66048]{1,0:T(8,128)} %get-tuple-element.76, s32[]{:T(128)} %bitcast.27, s32[]{:T(128)} %bitcast.28), dynamic_slice_sizes={1,33408} | dynamic-slice | bytes 267268 | tf_op jit(solution)/shard_map/vmap()/gather
  128.4 2.9 %dynamic-slice.7 = f32[1,33408]{1,0:T(1,128)S(1)} dynamic-slice(f32[16,66048]{1,0:T(8,128)} %get-tuple-element.76, s32[]{:T(128)} %bitcast.27, s32[]{:T(128)} %bitcast.28), dynamic_slice_sizes={1,33408} | dynamic-slice | bytes 267268 | tf_op jit(solution)/shard_map/vmap()/gather
  133.4 2.9 %dynamic-slice.7 = f32[1,33408]{1,0:T(1,128)S(1)} dynamic-slice(f32[16,66048]{1,0:T(8,128)} %get-tuple-element.76, s32[]{:T(128)} %bitcast.27, s32[]{:T(128)} %bitcast.28), dynamic_slice_sizes={1,33408} | dynamic-slice | bytes 267268 | tf_op jit(solution)/shard_map/vmap()/gather
  138.5 2.9 %dynamic-slice.7 = f32[1,33408]{1,0:T(1,128)S(1)} dynamic-slice(f32[16,66048]{1,0:T(8,128)} %get-tuple-element.76, s32[]{:T(128)} %bitcast.27, s32[]{:T(128)} %bitcast.28), dynamic_slice_sizes={1,33408} | dynamic-slice | bytes 267268 | tf_op jit(solution)/shard_map/vmap()/gather
  144.2 51.8 %all_to_all.30 = f32[16,256,128]{2,0,1:T(8,128)S(1)} all-to-all(f32[16,256,128]{2,0,1:T(8,128)S(1)} %copy_bitcast_fusion.1), channel_id=1, replica_groups=mesh['gy'=8,'gx'=4] {'gy'}, dimensions={1} | all-to-all | bytes 4194304 | tf_op jit(solution)/shard_map/all_to_all | solution.py:58
  196.8 38.8 %psum.7 = f32[2,128]{1,0:T(2,128)S(1)} all-reduce(f32[2,128]{1,0:T(2,128)S(1)} %pad_maximum_fusion.1), channel_id=1, replica_groups=mesh['gy'=8,'gx'=4] {'gy','gx'}, use_global_device_ids=true, to_apply=%region_4.5 | all-reduce | flops 256 | bytes 2048 | tf_op jit(solution)/shard_map/psum | solution.py:63
  236.2 1.9 copy.18
  (70 shorter events, 38.4 us)
Async XLA Ops:
  0.6 7.5 %copy-start = (s32[16]{0:T(128)S(1)}, s32[16]{0:T(128)}, u32[]{:S(2)}) copy-start(s32[16]{0:T(128)} %param.4) | copy-start | bytes 196
  0.6 7.7 %copy-start.1 = (f32[16]{0:T(128)S(1)}, f32[16]{0:T(128)}, u32[]{:S(2)}) copy-start(f32[16]{0:T(128)} %param.5) | copy-start | bytes 196
  0.6 55.8 %all-to-all-start = ((f32[128,32,128]{2,1,0:T(8,128)}), f32[128,32,128]{2,1,0:T(8,128)}, u32[]{:S(2)}, u32[]{:S(2)}) async-start(f32[128,32,128]{2,1,0:T(8,128)} %bitcast.34), calls=%async_computation | async-start | bytes 4194304 | tf_op jit(solution)/shard_map/all_to_all | solution.py:42
where the time goes:
time: 239 us; the launch traced here: 238 us
  blocking collectives  90.6 us (38%)
  local copies, waits for them, and re-layouts  86.5 us (36%)
  waiting for transfers between devices  47.9 us (20%)
  starting transfers between devices  7.42 us (3%)
  other arithmetic  4.58 us (2%)
    gather x64, local copies, waits for them, and re-layouts  80.9 us
    all_to_all x1, blocking collectives, on_device(): lax.all_to_all(moved, 'gy', split_axis=1, concat_axis=0, tiled=True)  51.8 us
    all_to_all x1, waiting for transfers between devices, on_device(): lax.all_to_all(stacked, 'gy', split_axis=0, concat_axis=1, tiled=True)  47.9 us
    psum x1, blocking collectives, on_device(): summed = lax.psum(partial_sums, ('gy', 'gx'))  38.8 us
    all_to_all x1, starting transfers between devices, on_device(): lax.all_to_all(stacked, 'gy', split_axis=0, concat_axis=1, tiled=True)  7.42 us
  transfers between devices with their start and end apart: 1, of which 1 were waited for; matrix products, arithmetic and copies ran while one was open for 0% of the time, Pallas kernels for 0%

commit v1 on v0

v1 whole, which is shorter than its diff:
```python
from functools import partial
import math

import jax
import jax.numpy as jnp
from jax import lax
from jax.experimental import pallas as pl
from jax.experimental.pallas import tpu as pltpu
from jax.sharding import PartitionSpec as P

MESH = pl.DeviceIdType.MESH
FIRST_FIELDS = (1, 2, 5, 6)
TILE = 32
PAD = TILE + 8


def taps_of(share):
    half = 0.5 * share * share
    bend = half * (1.0 - 2.0 * share / 3.0)
    right = (share - half - 3.0 * bend) * (1.0 / 12.0)
    left = (half - 3.0 * bend) * (1.0 / 12.0)
    return (
        -left,
        8.0 * left - right,
        8.0 * right + 6.0 * bend,
        1.0 - 8.0 * left - 6.0 * bend,
        left - 8.0 * right,
        right,
    )


def kernel(
    plan, shifts, fraction, fields, remapped, stress, held, moved, part, part_y,
    sums, part_x, send1, recv1, send2, recv2, ysend, yrecv, xsend, xrecv,
):
    n, m, components, chunks, depth, per_device, slab, azimuth, scale = plan
    me = lax.axis_index("gy")
    my_x = lax.axis_index("gx")
    order = FIRST_FIELDS + tuple(
        f for f in range(components) if f not in FIRST_FIELDS
    )

    def column_of(device):
        return device * per_device // components

    def field_of(device, chunk):
        if per_device >= components:
            return order[chunk]
        return lax.rem(lax.rem(device * per_device, components) + chunk + 1, components)

    def peer(step):
        return lax.rem(me + step, n)

    barrier = pltpu.get_barrier_semaphore()

    def greet_y(step, carry):
        pl.semaphore_signal(
            barrier, inc=1, device_id={"gy": peer(step)}, device_id_type=MESH
        )
        return carry

    lax.fori_loop(1, n, greet_y, 0)
    for step in range(1, m):
        pl.semaphore_signal(
            barrier,
            inc=1,
            device_id={"gx": lax.rem(my_x + step, m)},
            device_id_type=MESH,
        )

    def own_in(chunk):
        return pltpu.make_async_copy(
            fields.at[field_of(me, chunk), pl.ds(column_of(me), depth)],
            held[chunk].at[:, pl.ds(me * slab, slab)],
            recv1.at[chunk],
        )

    for chunk in range(chunks):
        own_in(chunk).start()
    pl.semaphore_wait(barrier, n - 1 + m - 1)

    for chunk in range(chunks):

        def send_in(step, carry):
            to = peer(step)
            pltpu.make_async_remote_copy(
                src_ref=fields.at[field_of(to, chunk), pl.ds(column_of(to), depth)],
                dst_ref=held[chunk].at[:, pl.ds(me * slab, slab)],
                send_sem=send1.at[chunk],
                recv_sem=recv1.at[chunk],
                device_id={"gy": to},
                device_id_type=MESH,
            ).start()
            return carry

        lax.fori_loop(1, n, send_in, 0)

    def whole(chunk):
        return held[chunk].at[:, pl.ds(0, azimuth)]

    def others(chunk):
        return held[chunk].at[:, pl.ds(0, azimuth - slab)]

    def remap(chunk):
        for c in range(depth):
            column = column_of(me) + c
            shift = shifts[column]
            taps = taps_of(fraction[column])
            held[chunk][c, pl.ds(azimuth, PAD)] = held[chunk][c, pl.ds(0, PAD)]

            def tile(t, carry):
                start = lax.rem(t * TILE - 3 - shift + 2 * azimuth, azimuth)
                total = None
                for k in range(6):
                    term = taps[k] * held[chunk][c, pl.ds(start + k, TILE)]
                    total = term if total is None else total + term
                moved[chunk, c, pl.ds(pl.multiple_of(t * TILE, TILE), TILE)] = total
                return carry

            lax.fori_loop(0, azimuth // TILE, tile, 0)

    def own_out(chunk):
        return pltpu.make_async_copy(
            moved.at[chunk, :, pl.ds(me * slab, slab)],
            remapped.at[field_of(me, chunk), pl.ds(column_of(me), depth)],
            recv2.at[chunk],
        )

    def pair_sum(chunk):
        def add(t, total):
            rows = pl.ds(pl.multiple_of(t * 8, 8), 8)
            for c in range(depth):
                total = total + moved[chunk, c, rows] * moved[chunk + 1, c, rows]
            return total

        total = lax.fori_loop(
            0, azimuth // 8, add, jnp.zeros((8, moved.shape[-1]), jnp.float32)
        )
        return jnp.sum(total, axis=0, keepdims=True)

    def start_sums():
        part[...] = jnp.zeros(part.shape, jnp.float32)
        if per_device >= components:
            part[0:1] = pair_sum(0)
            part[1:2] = -pair_sum(2)
        else:
            first = jnp.zeros((1, moved.shape[-1]), jnp.float32)
            second = first
            for chunk in range(0, chunks, 2):
                total = pair_sum(chunk)
                field = field_of(me, chunk)
                first = first + jnp.where(field == 1, total, 0.0)
                second = second - jnp.where(field == 5, total, 0.0)
            part[0:1] = first
            part[1:2] = second
        part_y[pl.ds(me, 1)] = part[...][None]

        def send_sum(step, carry):
            pltpu.make_async_remote_copy(
                src_ref=part,
                dst_ref=part_y.at[me],
                send_sem=ysend,
                recv_sem=yrecv,
                device_id={"gy": peer(step)},
                device_id_type=MESH,
            ).start()
            return carry

        lax.fori_loop(1, n, send_sum, 0)

    sums_at = min(3, chunks - 1) if per_device >= components else chunks - 1
    for chunk in range(chunks):
        pltpu.make_async_copy(whole(chunk), whole(chunk), recv1.at[chunk]).wait()
        remap(chunk)

        def send_out(step, carry):
            to = peer(step)
            pltpu.make_async_remote_copy(
                src_ref=moved.at[chunk, :, pl.ds(to * slab, slab)],
                dst_ref=remapped.at[field_of(me, chunk), pl.ds(column_of(me), depth)],
                send_sem=send2.at[chunk],
                recv_sem=recv2.at[chunk],
                device_id={"gy": to},
                device_id_type=MESH,
            ).start()
            return carry

        lax.fori_loop(1, n, send_out, 0)
        own_out(chunk).start()
        if chunk == sums_at:
            start_sums()

    few = part_y.at[pl.ds(0, n - 1)]
    pltpu.make_async_copy(few, few, yrecv).wait()
    pltpu.make_async_copy(few, few, ysend).wait()
    sums[...] = jnp.sum(part_y[...], axis=0)
    part_x[pl.ds(my_x, 1)] = sums[...][None]
    for step in range(1, m):
        pltpu.make_async_remote_copy(
            src_ref=sums,
            dst_ref=part_x.at[my_x],
            send_sem=xsend,
            recv_sem=xrecv,
            device_id={"gx": lax.rem(my_x + step, m)},
            device_id_type=MESH,
        ).start()
    rest = part_x.at[pl.ds(0, m - 1)]
    pltpu.make_async_copy(rest, rest, xrecv).wait()
    pltpu.make_async_copy(rest, rest, xsend).wait()
    stress[...] = jnp.sum(part_x[...], axis=0)[0:2] * scale

    for chunk in range(chunks):
        pltpu.make_async_copy(others(chunk), others(chunk), send1.at[chunk]).wait()
        pltpu.make_async_copy(others(chunk), others(chunk), send2.at[chunk]).wait()
        pltpu.make_async_copy(whole(chunk), whole(chunk), recv2.at[chunk]).wait()


def on_device(fields, shifts, fraction):
    components, columns, slab, vertical = fields.shape
    n = lax.axis_size("gy")
    m = lax.axis_size("gx")
    azimuth = slab * n
    per_device = components * columns // n
    chunks = min(per_device, components)
    depth = max(1, per_device // components)
    scale = 1.0 / math.sqrt(columns * m * azimuth)
    plan = (n, m, components, chunks, depth, per_device, slab, azimuth, scale)
    DMA = pltpu.SemaphoreType.DMA
    return pl.pallas_call(
        partial(kernel, plan),
        out_shape=(
            jax.ShapeDtypeStruct(fields.shape, jnp.float32),
            jax.ShapeDtypeStruct((2, vertical), jnp.float32),
        ),
        in_specs=[
            pl.BlockSpec(memory_space=pltpu.SMEM),
            pl.BlockSpec(memory_space=pltpu.SMEM),
            pl.BlockSpec(memory_space=pl.ANY),
        ],
        out_specs=(
            pl.BlockSpec(memory_space=pl.ANY),
            pl.BlockSpec(memory_space=pltpu.VMEM),
        ),
        scratch_shapes=[
            [pltpu.VMEM((depth, azimuth + PAD, vertical), jnp.float32)] * chunks,
            pltpu.VMEM((chunks, depth, azimuth, vertical), jnp.float32),
            pltpu.VMEM((8, vertical), jnp.float32),
            pltpu.VMEM((n, 8, vertical), jnp.float32),
            pltpu.VMEM((8, vertical), jnp.float32),
            pltpu.VMEM((m, 8, vertical), jnp.float32),
            DMA((chunks,)),
            DMA((chunks,)),
            DMA((chunks,)),
            DMA((chunks,)),
            DMA,
            DMA,
            DMA,
            DMA,
        ],
        compiler_params=pltpu.CompilerParams(collective_id=0, has_side_effects=True),
        cost_estimate=pl.CostEstimate(
            flops=12 * fields.size, bytes_accessed=8 * fields.size, transcendentals=0
        ),
    )(shifts, fraction, fields)


def solution(mesh):
    in_specs = (P(None, "gx", "gy", None), P("gx"), P("gx"))
    out_specs = (P(None, "gx", "gy", None), P())
    return jax.shard_map(
        on_device, mesh=mesh, in_specs=in_specs, out_specs=out_specs, check_vma=False
    )
```

time: 239 us -> 103 us (0.43)
  Pallas kernels: 0 us -> 98.6 us
  blocking collectives: 90.6 us -> 0 us
  local copies, waits for them, and re-layouts: 86.5 us -> 3.65 us
  waiting for transfers between devices: 47.9 us -> 0 us
  starting transfers between devices: 7.42 us -> 0 us
  other arithmetic: 4.58 us -> 0 us
    pallas_call x0 -> x1, Pallas kernels: none -> 98.6 us  [on_device(): pl.pallas_call(partial(kernel, plan), out_shape=(jax.ShapeDtypeStruct(fie...]
    gather x64 -> x0, local copies, waits for them, and re-layouts: 80.9 us -> none
    all_to_all x1 -> x0, blocking collectives: 51.8 us -> none  [on_device(): lax.all_to_all(moved, 'gy', split_axis=1, concat_axis=0, tiled=True)]
    all_to_all x1 -> x0, waiting for transfers between devices: 47.9 us -> none  [on_device(): lax.all_to_all(stacked, 'gy', split_axis=0, concat_axis=1, tiled=True)]
    psum x1 -> x0, blocking collectives: 38.8 us -> none  [on_device(): summed = lax.psum(partial_sums, ('gy', 'gx'))]
    all_to_all x1 -> x0, starting transfers between devices: 7.42 us -> none  [on_device(): lax.all_to_all(stacked, 'gy', split_axis=0, concat_axis=1, tiled=True)]
    all_to_all x2 -> x0, local copies, waits for them, and re-layouts: 2.47 us -> none  [the longest x1 1.79 us: on_device(): lax.all_to_all(stacked, 'gy', split_axis=0, concat_axis=1, tiled=True)]
  transfers between devices with their start and end apart: 1 -> 0, of which waited for: 1 -> 0; matrix products, arithmetic and copies ran while one was open for 0% -> 0% of each run, Pallas kernels for 0% -> 0%
where the time goes in v1:
time: 103 us
  Pallas kernels  98.6 us (96%)
  local copies, waits for them, and re-layouts  3.65 us (4%)
    pallas_call x1, Pallas kernels, on_device(): pl.pallas_call(partial(kernel, plan), out_shape=(jax.ShapeDtypeStruct(fie...  98.6 us
    unnamed x4, local copies, waits for them, and re-layouts  3.65 us

profile of v1, /device:TPU:0, one launch (start us, length us, event | category | flops | bytes accessed | tf_op | source)
XLA Modules:
  0.0 102.9 jit_solution(13571839676585612157)
XLA Ops:
  0.6 98.6 %shard_map.50 = (f32[8,16,32,128]{3,2,1,0:T(8,128)}, f32[2,128]{1,0:T(2,128)}) custom-call(s32[16]{0:T(128)} %shifts.1, f32[16]{0:T(128)} %fraction.1, f32[8,16,32,128]{3,2,1,0:T(8,128)} %fields.1), custom_call_target="tpu_custom_call" | custom-call | flops 6291456 | bytes 4194304 | tf_op jit(solution)/shard_map/pallas_call | solution.py:229
  99.2 0.0 copy-start
  99.2 3.1 %copy.7 = f32[8,16,32,128]{3,2,1,0:T(8,128)} copy(f32[8,16,32,128]{3,2,1,0:T(8,128)} %get-tuple-element.4) | data formatting | bytes 4194304
  102.3 0.0 copy-done
  102.3 0.6 copy.8
Async XLA Ops:
  99.2 3.1 %copy-start = (f32[2,128]{1,0:T(2,128)S(1)}, f32[2,128]{1,0:T(2,128)}, u32[]{:S(2)}) copy-start(f32[2,128]{1,0:T(2,128)} %get-tuple-element.5) | copy-start | bytes 3076

commit v2 on v1

--- a/solution.py
+++ b/solution.py
@@ -30,8 +30,9 @@
 
 
 def kernel(
-    plan, shifts, fraction, fields, remapped, stress, held, moved, part, part_y,
-    sums, part_x, send1, recv1, send2, recv2, ysend, yrecv, xsend, xrecv,
+    plan, shifts_in, fraction_in, fields, remapped, stress, held, moved, part, part_y,
+    sums, part_x, send1, recv1, send2, recv2, ysend, yrecv, xsend, xrecv, shifts,
+    fraction, small_sem,
 ):
     n, m, components, chunks, depth, per_device, slab, azimuth, scale = plan
     me = lax.axis_index("gy")
@@ -51,6 +52,10 @@
     def peer(step):
         return lax.rem(me + step, n)
 
+    small = (
+        pltpu.make_async_copy(shifts_in, shifts, small_sem.at[0]),
+        pltpu.make_async_copy(fraction_in, fraction, small_sem.at[1]),
+    )
     barrier = pltpu.get_barrier_semaphore()
 
     def greet_y(step, carry):
@@ -75,6 +80,8 @@
             recv1.at[chunk],
         )
 
+    for copy in small:
+        copy.start()
     for chunk in range(chunks):
         own_in(chunk).start()
     pl.semaphore_wait(barrier, n - 1 + m - 1)
@@ -168,6 +175,8 @@
 
         lax.fori_loop(1, n, send_sum, 0)
 
+    for copy in small:
+        copy.wait()
     sums_at = min(3, chunks - 1) if per_device >= components else chunks - 1
     for chunk in range(chunks):
         pltpu.make_async_copy(whole(chunk), whole(chunk), recv1.at[chunk]).wait()
@@ -233,9 +242,9 @@
             jax.ShapeDtypeStruct((2, vertical), jnp.float32),
         ),
         in_specs=[
-            pl.BlockSpec(memory_space=pltpu.SMEM),
-            pl.BlockSpec(memory_space=pltpu.SMEM),
-            pl.BlockSpec(memory_space=pl.ANY),
+            pl.BlockSpec(memory_space=pltpu.HBM),
+            pl.BlockSpec(memory_space=pltpu.HBM),
+            pl.BlockSpec(memory_space=pltpu.HBM),
         ],
         out_specs=(
             pl.BlockSpec(memory_space=pl.ANY),
@@ -256,12 +265,17 @@
             DMA,
             DMA,
             DMA,
+            pltpu.SMEM((columns,), jnp.int32),
+            pltpu.SMEM((columns,), jnp.float32),
+            DMA((2,)),
         ],
-        compiler_params=pltpu.CompilerParams(collective_id=0, has_side_effects=True),
+        compiler_params=pltpu.CompilerParams(
+            collective_id=0, has_side_effects=True, vmem_limit_bytes=16 * 2**20
+        ),
         cost_estimate=pl.CostEstimate(
             flops=12 * fields.size, bytes_accessed=8 * fields.size, transcendentals=0
         ),
-    )(shifts, fraction, fields)
+    )(*(pltpu.with_memory_space_constraint(a, pltpu.HBM) for a in (shifts, fraction, fields)))
 
 
 def solution(mesh):

time: 103 us -> 99.9 us (0.970)
  local copies, waits for them, and re-layouts: 3.65 us -> 1.88 us
  Pallas kernels: 98.6 us -> 97.3 us
    unnamed x4 -> x2, local copies, waits for them, and re-layouts: 3.65 us -> 1.88 us
    pallas_call x1, Pallas kernels: 98.6 us -> 97.3 us  [on_device(): pl.pallas_call(partial(kernel, plan), out_shape=(jax.ShapeDtypeStruct(fie...]
where the time goes in v2:
time: 99.9 us; the launch traced here: 99.8 us
  Pallas kernels  97.3 us (97%)
  local copies, waits for them, and re-layouts  1.88 us (2%)
    pallas_call x1, Pallas kernels, on_device(): pl.pallas_call(partial(kernel, plan), out_shape=(jax.ShapeDtypeStruct(fie...  97.3 us

profile of v2, /device:TPU:0, one launch (start us, length us, event | category | flops | bytes accessed | tf_op | source)
XLA Modules:
  0.0 99.8 jit_solution(7670547692716183007)
XLA Ops:
  0.6 97.3 %shard_map.50 = (f32[8,16,32,128]{3,2,1,0:T(8,128)S(1)}, f32[2,128]{1,0:T(2,128)S(1)}) custom-call(s32[16]{0:T(128)} %shifts_in.1, f32[16]{0:T(128)} %fraction_in.1, f32[8,16,32,128]{3,2,1,0:T(8,128)} %fields.1), custom_call_target="tpu_custom_call" | custom-call | flops 6291456 | bytes 4194304 | tf_op jit(solution)/shard_map/pallas_call | solution.py:238
  97.9 1.3 %copy.7 = f32[8,16,32,128]{3,2,1,0:T(8,128)} copy(f32[8,16,32,128]{3,2,1,0:T(8,128)S(1)} %get-tuple-element.4) | data formatting | bytes 4194304
  99.2 0.6 copy.8

commit v3 on v2

--- a/solution.py
+++ b/solution.py
@@ -50,7 +50,8 @@
         return lax.rem(lax.rem(device * per_device, components) + chunk + 1, components)
 
     def peer(step):
-        return lax.rem(me + step, n)
+        away = lax.div(step, 2) * (1 - 2 * lax.rem(step, 2))
+        return lax.rem(me + n // 2 + away, n)
 
     small = (
         pltpu.make_async_copy(shifts_in, shifts, small_sem.at[0]),
@@ -146,7 +147,6 @@
         return jnp.sum(total, axis=0, keepdims=True)
 
     def start_sums():
-        part[...] = jnp.zeros(part.shape, jnp.float32)
         if per_device >= components:
             part[0:1] = pair_sum(0)
             part[1:2] = -pair_sum(2)
@@ -216,7 +216,7 @@
     rest = part_x.at[pl.ds(0, m - 1)]
     pltpu.make_async_copy(rest, rest, xrecv).wait()
     pltpu.make_async_copy(rest, rest, xsend).wait()
-    stress[...] = jnp.sum(part_x[...], axis=0)[0:2] * scale
+    stress[...] = jnp.sum(part_x[...], axis=0) * scale
 
     for chunk in range(chunks):
         pltpu.make_async_copy(others(chunk), others(chunk), send1.at[chunk]).wait()
@@ -253,10 +253,10 @@
         scratch_shapes=[
             [pltpu.VMEM((depth, azimuth + PAD, vertical), jnp.float32)] * chunks,
             pltpu.VMEM((chunks, depth, azimuth, vertical), jnp.float32),
-            pltpu.VMEM((8, vertical), jnp.float32),
-            pltpu.VMEM((n, 8, vertical), jnp.float32),
-            pltpu.VMEM((8, vertical), jnp.float32),
-            pltpu.VMEM((m, 8, vertical), jnp.float32),
+            pltpu.VMEM((2, vertical), jnp.float32),
+            pltpu.VMEM((n, 2, vertical), jnp.float32),
+            pltpu.VMEM((2, vertical), jnp.float32),
+            pltpu.VMEM((m, 2, vertical), jnp.float32),
             DMA((chunks,)),
             DMA((chunks,)),
             DMA((chunks,)),

time: 99.9 us -> 101 us (1.011)
  no operation moved by 1% of the time
where the time goes in v3:
time: 101 us; the launch traced here: 100 us
  Pallas kernels  97.9 us (97%)
  local copies, waits for them, and re-layouts  1.88 us (2%)
    pallas_call x1, Pallas kernels, on_device(): pl.pallas_call(partial(kernel, plan), out_shape=(jax.ShapeDtypeStruct(fie...  97.9 us

profile of v3, /device:TPU:0, one launch (start us, length us, event | category | flops | bytes accessed | tf_op | source)
XLA Modules:
  0.0 100.5 jit_solution(18010425603907617706)
XLA Ops:
  0.6 97.9 %shard_map.50 = (f32[8,16,32,128]{3,2,1,0:T(8,128)S(1)}, f32[2,128]{1,0:T(2,128)S(1)}) custom-call(s32[16]{0:T(128)} %shifts_in.1, f32[16]{0:T(128)} %fraction_in.1, f32[8,16,32,128]{3,2,1,0:T(8,128)} %fields.1), custom_call_target="tpu_custom_call" | custom-call | flops 6291456 | bytes 4194304 | tf_op jit(solution)/shard_map/pallas_call | solution.py:238
  98.6 1.3 %copy.7 = f32[8,16,32,128]{3,2,1,0:T(8,128)} copy(f32[8,16,32,128]{3,2,1,0:T(8,128)S(1)} %get-tuple-element.4) | data formatting | bytes 4194304
  99.9 0.6 copy.8

commit v4 on v3

--- a/solution.py
+++ b/solution.py
@@ -224,6 +224,18 @@
         pltpu.make_async_copy(whole(chunk), whole(chunk), recv2.at[chunk]).wait()
 
 
+def write_out(landed, sums, remapped, stress, done):
+    copies = [
+        pltpu.make_async_copy(landed.at[f], remapped.at[f], done.at[f])
+        for f in range(landed.shape[0])
+    ]
+    copies.append(pltpu.make_async_copy(sums, stress, done.at[landed.shape[0]]))
+    for copy in copies:
+        copy.start()
+    for copy in copies:
+        copy.wait()
+
+
 def on_device(fields, shifts, fraction):
     components, columns, slab, vertical = fields.shape
     n = lax.axis_size("gy")
@@ -235,7 +247,7 @@
     scale = 1.0 / math.sqrt(columns * m * azimuth)
     plan = (n, m, components, chunks, depth, per_device, slab, azimuth, scale)
     DMA = pltpu.SemaphoreType.DMA
-    return pl.pallas_call(
+    landed, sums = pl.pallas_call(
         partial(kernel, plan),
         out_shape=(
             jax.ShapeDtypeStruct(fields.shape, jnp.float32),
@@ -276,6 +288,20 @@
             flops=12 * fields.size, bytes_accessed=8 * fields.size, transcendentals=0
         ),
     )(*(pltpu.with_memory_space_constraint(a, pltpu.HBM) for a in (shifts, fraction, fields)))
+    return pl.pallas_call(
+        write_out,
+        out_shape=(
+            jax.ShapeDtypeStruct(fields.shape, jnp.float32),
+            jax.ShapeDtypeStruct((2, vertical), jnp.float32),
+        ),
+        in_specs=[pl.BlockSpec(memory_space=pl.ANY)] * 2,
+        out_specs=(pl.BlockSpec(memory_space=pl.ANY),) * 2,
+        scratch_shapes=[DMA((components + 1,))],
+        compiler_params=pltpu.CompilerParams(vmem_limit_bytes=16 * 2**20),
+        cost_estimate=pl.CostEstimate(
+            flops=0, bytes_accessed=8 * fields.size, transcendentals=0
+        ),
+    )(landed, sums)
 
 
 def solution(mesh):

time: 101 us -> 100 us (0.990)
  local copies, waits for them, and re-layouts: 1.88 us -> 0 us
  Pallas kernels: 97.9 us -> 99.3 us
    unnamed x2 -> x0, local copies, waits for them, and re-layouts: 1.88 us -> none
    pallas_call x0 -> x1, Pallas kernels: none -> 1.39 us  [on_device(): pl.pallas_call(write_out, out_shape=(jax.ShapeDtypeStruct(fields.shape, j...]
where the time goes in v4:
time: 100 us
  Pallas kernels  99.3 us (99%)
    pallas_call x1, Pallas kernels, on_device(): pl.pallas_call(partial(kernel, plan), out_shape=(jax.ShapeDtypeStruct(fie...  97.9 us

profile of v4, /device:TPU:0, one launch (start us, length us, event | category | flops | bytes accessed | tf_op | source)
XLA Modules:
  0.0 100.0 jit_solution(15737154343446887842)
XLA Ops:
  0.6 97.9 %shard_map.50 = (f32[8,16,32,128]{3,2,1,0:T(8,128)S(1)}, f32[2,128]{1,0:T(2,128)S(1)}) custom-call(s32[16]{0:T(128)} %shifts_in.1, f32[16]{0:T(128)} %fraction_in.1, f32[8,16,32,128]{3,2,1,0:T(8,128)} %fields.1), custom_call_target="tpu_custom_call" | custom-call | flops 6291456 | bytes 4194304 | tf_op jit(solution)/shard_map/pallas_call | solution.py:250
  98.6 1.4 %shard_map.51 = (f32[8,16,32,128]{3,2,1,0:T(8,128)}, f32[2,128]{1,0:T(2,128)}) custom-call(f32[8,16,32,128]{3,2,1,0:T(8,128)S(1)} %get-tuple-element.4.landed, f32[2,128]{1,0:T(2,128)S(1)} %get-tuple-element.5.sums), custom_call_target="tpu_custom_call" | custom-call | bytes 4194304 | tf_op jit(solution)/shard_map/pallas_call | solution.py:291
